TPU v7x, 32 devices: a whole 2x2x4 slice. The times are simulated.
32 devices in a mesh: replica: 4 (over y, x), fsdp: 8 (over z, core).
Axes of the slice: x: 2, y: 2, z: 4, core: 2. Of those that a mesh axis runs over, the one named last changes fastest.
Arguments:
- codes: int32 [4, 8192, 4096], P('replica', None, 'fsdp'), may hold values from -127 to 127
- scales: float32 [4, 32, 8192], P('replica', 'fsdp'), may hold values from 0.002 to 0.03
- master: float32 [8192, 4096], P(('replica', 'fsdp')), may hold values from -6 to 6
- momentum: float32 [8192, 4096], P(('replica', 'fsdp')), may hold values from -6 to 6
Outputs:
- new_master: float32 [8192, 4096], P(('replica', 'fsdp'))
- new_momentum: float32 [8192, 4096], P(('replica', 'fsdp'))
- weights: bfloat16 [8192, 4096], P(None, 'fsdp')
All inputs are finite; a program needn't handle non-finite values.
Results may differ from a plain program's by a relative error of at most 0.0075.
Values may be sent and summed in bfloat16 or wider, within the bound.
A program may use at most 128 MiB of HBM per device.

v0:
```python
import jax
import jax.numpy as jnp
from jax import lax
from jax.sharding import PartitionSpec as P

outer_rate = 0.7
momentum_factor = 0.9


def dequantize(codes, scales):
    block_count = scales.shape[1]
    total_rows = codes.shape[1]
    width = codes.shape[2]
    scaled = codes[0].astype(jnp.float32).reshape(total_rows, block_count, width // block_count)
    return (scaled * jnp.transpose(scales[0])[:, :, None]).reshape(total_rows, width)


def outer_update(summed, master, momentum, replica_count):
    mean_delta = summed / replica_count
    new_momentum = momentum_factor * momentum + mean_delta
    new_master = master - outer_rate * (mean_delta + momentum_factor * new_momentum)
    return (new_master, new_momentum)


def local(codes, scales, master, momentum):
    replica_count = lax.axis_size("replica")
    delta_local = dequantize(codes, scales)
    partial_sum = lax.psum_scatter(
        delta_local.astype(jnp.bfloat16), "replica", scatter_dimension=0, tiled=True
    ).astype(jnp.float32)
    summed = lax.all_to_all(
        partial_sum.astype(jnp.bfloat16), "fsdp", split_axis=0, concat_axis=1, tiled=True
    ).astype(partial_sum.dtype)
    new_master, new_momentum = outer_update(summed, master, momentum, replica_count)
    rounded = new_master.astype(jnp.bfloat16)
    columns = lax.all_to_all(rounded, "fsdp", split_axis=1, concat_axis=0, tiled=True)
    weights = lax.all_gather(columns, "replica", axis=0, tiled=True)
    return (new_master, new_momentum, weights)


def solution(mesh):
    return jax.shard_map(
        local,
        mesh=mesh,
        in_specs=(
            P("replica", None, "fsdp"),
            P("replica", "fsdp", None),
            P(("replica", "fsdp"), None),
            P(("replica", "fsdp"), None),
        ),
        out_specs=(P(("replica", "fsdp"), None), P(("replica", "fsdp"), None), P(None, "fsdp")),
        check_vma=False,
    )
```

profile of v0, /device:TPU:0, one launch (start us, length us, event | category | flops | bytes accessed | tf_op | source)
XLA Modules:
  0.0 348.3 jit_solution(17330387453719186282)
XLA Ops:
  7.2 0.0 reduce-scatter.2.cloned.1.call-start
  7.2 3.5 %copy.12 = f32[8192,4]{1,0:T(8,128)} copy(f32[8192,4]{0,1:T(4,128)} %bitcast.31) | data formatting | bytes 262144 | tf_op jit(solution)/shard_map/transpose | solution.py:15
  10.7 15.9 %mul.23 = f32[8192,4,128]{2,1,0:T(4,128)S(1)} broadcast(f32[8192,4]{1,0:T(8,128)} %copy.12), dimensions={0,1} | broadcast | bytes 16908288 | tf_op jit(solution)/shard_map/mul | solution.py:15
  26.6 11.6 %fusion = bf16[8192,512]{1,0:T(8,128)(2,1)} fusion(f32[1024,8,4,128]{3,2,1,0:T(4,128)S(1)} %bitcast.26, s32[1,8192,512]{2,1,0:T(8,128)} %param.4), kind=kLoop, calls=%fused_computation.1 | loop fusion | flops 12582912 | bytes 41943040 | tf_op jit(solution)/shard_map/convert_element_type | solution.py:29
  38.2 0.0 reduce-scatter.2.cloned.1.call-update
  38.3 89.2 %reduce-scatter.2.cloned.1.call-done = bf16[2048,512]{1,0:T(8,128)(2,1)} async-done(((bf16[8192,512]{1,0:T(8,128)(2,1)}), bf16[2048,512]{1,0:T(8,128)(2,1)}) %reduce-scatter.2.cloned.1.call-update) | async-done | bytes 2097168 | tf_op jit(solution)/shard_map/reduce_scatter | solution.py:28
  127.5 4.6 %all-to-all-start = ((bf16[8,256,512]{2,1,0:T(8,128)(2,1)}), bf16[8,256,512]{2,1,0:T(8,128)(2,1)S(1)}, u32[]{:S(2)}, u32[]{:S(2)}) async-start(bf16[8,256,512]{2,1,0:T(8,128)(2,1)} %bitcast.30), calls=%async_computation.1 | async-start | bytes 4194304 | tf_op jit(solution)/shard_map/all_to_all | solution.py:31
  132.1 0.0 all-gather.2.cloned.1.call-start
  132.1 5.6 %copy.14 = f32[256,4096]{0,1:T(8,128)} copy(f32[256,4096]{1,0:T(8,128)} %param.7) | data formatting | bytes 8388608 | tf_op args[3]
  137.7 5.6 %copy.15 = f32[256,4096]{0,1:T(8,128)} copy(f32[256,4096]{1,0:T(8,128)} %param.6) | data formatting | bytes 8388608 | tf_op args[2]
  143.3 37.8 %all-to-all-done = bf16[8,256,512]{2,1,0:T(8,128)(2,1)S(1)} async-done(((bf16[8,256,512]{2,1,0:T(8,128)(2,1)}), bf16[8,256,512]{2,1,0:T(8,128)(2,1)S(1)}, u32[]{:S(2)}, u32[]{:S(2)}) %all-to-all-start) | async-done | bytes 2097184 | tf_op jit(solution)/shard_map/all_to_all | solution.py:31
  181.1 2.4 copy.13
  183.5 0.0 copy-start
  183.5 2.1 convert_multiply_fusion
  185.6 0.7 copy-done
  186.3 7.3 %fusion.3 = (bf16[256,4096]{0,1:T(8,128)(2,1)}, f32[256,4096]{0,1:T(8,128)}, f32[256,4096]{0,1:T(8,128)}) fusion(f32[256,4096]{0,1:T(8,128)} %copy.15, f32[256,4096]{0,1:T(8,128)S(1)} %copy-done, f32[8,256,512]{1,2,0:T(8,128)S(1)} %convert_multiply_fusion), kind=kLoop, calls=%fused_computation.7 | loop fusion | flops 7340032 | bytes 23068672 | tf_op jit(solution)/shard_map/convert_element_type | solution.py:35
  193.5 52.5 %all_to_all.32 = bf16[256,8,512]{0,2,1:T(8,128)(2,1)S(1)} all-to-all(bf16[256,8,512]{0,2,1:T(8,128)(2,1)} %bitcast.29), channel_id=1, replica_groups=mesh['replica'=4,'fsdp'=8] {'fsdp'}, dimensions={1} | all-to-all | bytes 4194304 | tf_op jit(solution)/shard_map/all_to_all | solution.py:36
  246.1 2.4 copy.16
  248.5 0.0 all-gather.2.cloned.1.call-update
  248.5 5.6 %copy.17 = f32[256,4096]{1,0:T(8,128)} copy(f32[256,4096]{0,1:T(8,128)} %get-tuple-element.7) | data formatting | bytes 8388608
  254.1 6.0 %copy.18 = f32[256,4096]{1,0:T(8,128)} copy(f32[256,4096]{0,1:T(8,128)} %get-tuple-element.8) | data formatting | bytes 8388608
  260.1 74.0 %all-gather.2.cloned.1.call-done = bf16[8192,512]{1,0:T(8,128)(2,1)} async-done(((bf16[2048,512]{1,0:T(8,128)(2,1)}), bf16[8192,512]{1,0:T(8,128)(2,1)}) %all-gather.2.cloned.1.call-update) | async-done | bytes 8388624 | tf_op jit(solution)/shard_map/all_gather | solution.py:37
  334.1 7.3 %copy.22 = bf16[8192,512]{1,0:T(8,128)(2,1)} copy(bf16[8192,512]{1,0:T(8,128)(2,1)} %all-gather.2.cloned.1.call-done) | data formatting | bytes 16777216
Async XLA Ops:
  7.2 120.3 %reduce-scatter.2.cloned.1.call-start = ((), (), s32[]{:S(2)}) async-start(), calls=%async_computation.3 | async-start | bytes 10485760 | tf_op jit(solution)/shard_map/reduce_scatter | solution.py:28
  127.5 53.7 %all-to-all-start = ((bf16[8,256,512]{2,1,0:T(8,128)(2,1)}), bf16[8,256,512]{2,1,0:T(8,128)(2,1)S(1)}, u32[]{:S(2)}, u32[]{:S(2)}) async-start(bf16[8,256,512]{2,1,0:T(8,128)(2,1)} %bitcast.30), calls=%async_computation.1 | async-start | bytes 4194304 | tf_op jit(solution)/shard_map/all_to_all | solution.py:31
  132.1 202.0 %all-gather.2.cloned.1.call-start = ((), (), s32[]{:S(2)}) async-start(), calls=%async_computation.4 | async-start | bytes 10485760 | tf_op jit(solution)/shard_map/all_gather | solution.py:37
  183.5 2.8 copy-start
Sparse Core Ops, SparseCore 0:
  38.4 89.0 reduce-scatter.1
  248.6 85.4 all-gather.1
where the time goes:
time: 349 us; the launch traced here: 348 us
  waiting for transfers between devices  201 us (58%)
  local copies, waits for them, and re-layouts  55 us (16%)
  blocking collectives  52.5 us (15%)
  other arithmetic  21 us (6%)
  between operations  14.1 us (4%)
  starting transfers between devices  4.69 us (1%)
    reduce_scatter x1, waiting for transfers between devices, local(): lax.psum_scatter(delta_local.astype(jnp.bfloat16), 'replica', scatter_dim...  89.2 us
    all_gather x1, waiting for transfers between devices, local(): weights = lax.all_gather(columns, 'replica', axis=0, tiled=True)  74 us
    all_to_all x1, blocking collectives, local(): lax.all_to_all(rounded, 'fsdp', split_axis=1, concat_axis=0, tiled=True)  52.5 us
    all_to_all x1, waiting for transfers between devices, local(): lax.all_to_all(partial_sum.astype(jnp.bfloat16), 'fsdp', split_axis=0, co...  37.8 us
    unnamed x7, local copies, waits for them, and re-layouts  30.8 us
    mul x1, local copies, waits for them, and re-layouts, dequantize(): scaled * jnp.transpose(scales[0])[:, :, None]  15.9 us
    convert_element_type x1, other arithmetic, local(): delta_local.astype(jnp.bfloat16)  11.6 us
    convert_element_type x1, other arithmetic, local(): rounded = new_master.astype(jnp.bfloat16)  7.26 us
  transfers between devices with their start and end apart: 3, of which 3 were waited for; matrix products, arithmetic and copies ran while one was open for 7% of the time, Pallas kernels for 0%

commit v1 on v0

v1 whole, which is shorter than its diff:
```python
import functools

import jax
import jax.numpy as jnp
from jax import lax
from jax.experimental import pallas as pl
from jax.experimental.pallas import tpu as pltpu
from jax.sharding import PartitionSpec as P

MESH = pl.DeviceIdType.MESH

outer_rate = 0.7
momentum_factor = 0.9

LAGS = (0, 2, 3, 4, 5, 6, 7)
RS1, RS2, X1, X2, AG1, AG2 = range(6)


def kernel(cfg, codes, scales, master, momentum, new_master, new_momentum, weights,
           delta, rs1e, rs1o, rs2e, rs2o, part, got, wsend, wbuf, mast, mom, cbuf, sbuf,
           send_sem, recv_sem, in_sem, state_sem, out_sem):
    A, B, F, K, sub, width, blocks = cfg
    R, FS, block = A * B, F * sub, width // blocks
    r, f = lax.axis_index("replica"), lax.axis_index("fsdp")
    a, b = r // B, lax.rem(r, B)

    def a_peer(i):
        return lax.rem(a + 1 + i, A)

    def b_peer(i):
        return lax.rem(b + 1 + i, B)

    def f_peer(i):
        return lax.rem(f + 1 + i, F)

    def load(k):
        slot = lax.rem(k, 2)
        return (
            pltpu.make_async_copy(codes.at[:, k], cbuf.at[slot], in_sem.at[0, slot]),
            pltpu.make_async_copy(scales.at[:, k], sbuf.at[slot], in_sem.at[1, slot]),
        )

    for k in range(min(2, K)):
        for copy in load(k):
            copy.start()
    state_in = (
        pltpu.make_async_copy(master, mast, state_sem.at[0]),
        pltpu.make_async_copy(momentum, mom, state_sem.at[1]),
    )
    for copy in state_in:
        copy.start()

    barrier = pltpu.get_barrier_semaphore()
    for i in range(A - 1):
        pl.semaphore_signal(barrier, inc=1, device_id=(a_peer(i) * B + b, f), device_id_type=MESH)
    for i in range(B - 1):
        pl.semaphore_signal(barrier, inc=1, device_id=(a * B + b_peer(i), f), device_id_type=MESH)
    for i in range(F - 1):
        pl.semaphore_signal(barrier, inc=1, device_id=(r, f_peer(i)), device_id_type=MESH)
    pl.semaphore_wait(barrier, A + B + F - 3)

    def send(stage, k, src, dst, device):
        pltpu.make_async_remote_copy(
            src_ref=src, dst_ref=dst, send_sem=send_sem.at[stage, k], recv_sem=recv_sem.at[stage, k],
            device_id=device, device_id_type=MESH,
        ).start()

    def wait_bytes(sem, stage, k, ref):
        pltpu.make_async_copy(ref, ref, sem.at[stage, k]).wait()

    def rows(j):
        return pl.ds(pl.multiple_of(j * sub, sub), sub)

    def f32(x):
        return x.astype(jnp.float32)

    def amount(stage, k, even):
        if stage == RS1:
            return rs1e.at[k // 2] if even else rs1o.at[k // 2]
        if stage == RS2:
            return rs2e.at[k // 2] if even else rs2o.at[k // 2]
        if stage in (X1, X2):
            return part.at[k, pl.ds(0, (F - 1) * sub)]
        first, second = (B - 1, B * (A - 1)) if even else (A - 1, A * (B - 1))
        count = first if stage == AG1 else second
        return delta.at[k, pl.ds(0, count)]

    def by_parity(k, fn):
        @pl.when(lax.rem(k, 2) == 0)
        def _():
            fn(True)

        if K > 1:
            @pl.when(lax.rem(k, 2) == 1)
            def _():
                fn(False)

    def stage0(k):
        slot = lax.rem(k, 2)
        for copy in load(k):
            copy.wait()

        def one(g, carry):
            q, j = g // F, lax.rem(g, F)
            for n in range(blocks):
                cols = pl.ds(n * block, block)
                value = f32(cbuf[slot, g, :, cols]) * sbuf[slot, g, :, pl.ds(n, 1)]
                delta[k, q, rows(j), cols] = value.astype(jnp.bfloat16)
            return carry

        lax.fori_loop(0, R * F, one, 0)

        @pl.when(k + 2 < K)
        def _():
            for copy in load(k + 2):
                copy.start()

        def go(even):
            if even:
                for i in range(B - 1):
                    bb = b_peer(i)
                    for aa in range(A):
                        send(RS1, k, delta.at[k, aa * B + bb], rs1e.at[k // 2, B - 2 - i, aa], (a * B + bb, f))
            else:
                for i in range(A - 1):
                    aa = a_peer(i)
                    send(RS1, k, delta.at[k, pl.ds(aa * B, B)], rs1o.at[k // 2, A - 2 - i], (aa * B + b, f))

        by_parity(k, go)

    def stage1(k):
        def go(even):
            wait_bytes(recv_sem, RS1, k, amount(RS1, k, even))
            buf, count, peers = (rs1e, B - 1, A - 1) if even else (rs1o, A - 1, B - 1)
            for i in range(peers):
                q = a_peer(i) if even else b_peer(i)
                target = q * B + b if even else a * B + q

                def add(j, carry):
                    total = f32(delta[k, target, rows(j), :])
                    for s in range(count):
                        total = total + f32(buf[k // 2, s, q, rows(j), :])
                    buf[k // 2, 0, q, rows(j), :] = total.astype(jnp.bfloat16)
                    return carry

                lax.fori_loop(0, F, add, 0)
                dst = rs2e if even else rs2o
                send(RS2, k, buf.at[k // 2, 0, q], dst.at[k // 2, peers - 1 - i], (target, f))

        by_parity(k, go)

    def stage2(k):
        def go(even):
            wait_bytes(recv_sem, RS2, k, amount(RS2, k, even))
            one, two = (rs1e, rs2e) if even else (rs1o, rs2o)
            ones, twos = (B - 1, A - 1) if even else (A - 1, B - 1)
            q = a if even else b

            def add(j, carry):
                total = f32(delta[k, r, rows(j), :])
                for s in range(ones):
                    total = total + f32(one[k // 2, s, q, rows(j), :])
                for s in range(twos):
                    total = total + f32(two[k // 2, s, rows(j), :])
                part[k, rows(j), :] = total.astype(jnp.bfloat16)
                return carry

            lax.fori_loop(0, F, add, 0)

        by_parity(k, go)

        def out(i, carry):
            j = f_peer(i)
            send(X1, k, part.at[k, rows(j)], got.at[k, rows(f)], (r, j))
            return carry

        lax.fori_loop(0, F - 1, out, 0)
        got[k, rows(f), :] = part[k, rows(f), :]

    def results(k):
        span = pl.ds(pl.multiple_of(k * sub, sub), sub)
        return (
            pltpu.make_async_copy(mast.at[span], new_master.at[span], out_sem.at[0, k]),
            pltpu.make_async_copy(mom.at[span], new_momentum.at[span], out_sem.at[1, k]),
        )

    def stage3(k):
        @pl.when(k == 0)
        def _():
            for copy in state_in:
                copy.wait()

        wait_bytes(recv_sem, X1, k, amount(X1, k, True))
        span = pl.ds(pl.multiple_of(k * sub, sub), sub)

        def update(j, carry):
            cols = pl.ds(pl.multiple_of(j * width, width), width)
            mean = f32(got[k, rows(j), :]) * (1.0 / R)
            m = momentum_factor * mom[span, cols] + mean
            p = mast[span, cols] - outer_rate * (mean + momentum_factor * m)
            mom[span, cols] = m
            mast[span, cols] = p
            wsend[k, rows(j), :] = p.astype(jnp.bfloat16)
            return carry

        lax.fori_loop(0, F, update, 0)

        def out(i, carry):
            j = f_peer(i)
            send(X2, k, wsend.at[k, rows(j)], wbuf.at[k, r, rows(f)], (r, j))
            return carry

        lax.fori_loop(0, F - 1, out, 0)
        wbuf[k, r, rows(f), :] = wsend[k, rows(f), :]
        for copy in results(k):
            copy.start()

    def stage4(k):
        wait_bytes(recv_sem, X2, k, amount(X2, k, True))

        def go(even):
            here = wbuf.at[k, r]
            for i in range(B - 1 if even else A - 1):
                target = a * B + b_peer(i) if even else a_peer(i) * B + b
                send(AG1, k, here, here, (target, f))

        by_parity(k, go)

    def stage5(k):
        def go(even):
            wait_bytes(recv_sem, AG1, k, amount(AG1, k, even))
            if even:
                here = wbuf.at[k, pl.ds(a * B, B)]
                for i in range(A - 1):
                    send(AG2, k, here, here, (a_peer(i) * B + b, f))
            else:
                for i in range(B - 1):
                    for aa in range(A):
                        here = wbuf.at[k, aa * B + b]
                        send(AG2, k, here, here, (a * B + b_peer(i), f))

        by_parity(k, go)

    def columns(k, q):
        return pltpu.make_async_copy(
            wbuf.at[k, q].reshape(F, sub, width), weights.at[pl.ds(q * F, F), k], out_sem.at[2 + q, k]
        )

    def stage6(k):
        by_parity(k, lambda even: wait_bytes(recv_sem, AG2, k, amount(AG2, k, even)))
        for q in range(R):
            columns(k, q).start()

    stages = (stage0, stage1, stage2, stage3, stage4, stage5, stage6)

    def step(t, carry):
        for lag, stage in zip(LAGS, stages):
            k = t - lag

            @pl.when((k >= 0) & (k < K))
            def _():
                stage(k)

        return carry

    lax.fori_loop(0, K + LAGS[-1], step, 0)

    def finish(k, carry):
        for copy in results(k):
            copy.wait()
        for q in range(R):
            columns(k, q).wait()

        def go(even):
            for stage in range(6):
                wait_bytes(send_sem, stage, k, amount(stage, k, even))

        by_parity(k, go)
        return carry

    lax.fori_loop(0, K, finish, 0)


def solution(mesh):
    R, F = mesh.shape["replica"], mesh.shape["fsdp"]
    B = 2
    A = R // B

    def local(codes, scales, master, momentum):
        total_rows, width = codes.shape[1:]
        blocks = scales.shape[1]
        own = total_rows // (R * F)
        sub = 32 if own % 32 == 0 else own
        K = own // sub
        FS = F * sub
        even, odd = (K + 1) // 2, max(1, K // 2)
        codes = codes.reshape(R * F, K, sub, width)
        scales = jnp.transpose(scales[0]).reshape(R * F, K, sub, blocks)
        any_spec = pl.BlockSpec(memory_space=pl.ANY)
        bf16 = jnp.bfloat16
        new_master, new_momentum, weights = pl.pallas_call(
            functools.partial(kernel, (A, B, F, K, sub, width, blocks)),
            out_shape=(
                jax.ShapeDtypeStruct(master.shape, jnp.float32),
                jax.ShapeDtypeStruct(momentum.shape, jnp.float32),
                jax.ShapeDtypeStruct((R * F, K, sub, width), bf16),
            ),
            in_specs=[any_spec] * 4,
            out_specs=(any_spec,) * 3,
            scratch_shapes=[
                pltpu.VMEM((K, R, FS, width), bf16),
                pltpu.VMEM((even, B - 1, A, FS, width), bf16),
                pltpu.VMEM((odd, A - 1, B, FS, width), bf16),
                pltpu.VMEM((even, A - 1, FS, width), bf16),
                pltpu.VMEM((odd, B - 1, FS, width), bf16),
                pltpu.VMEM((K, FS, width), bf16),
                pltpu.VMEM((K, FS, width), bf16),
                pltpu.VMEM((K, FS, width), bf16),
                pltpu.VMEM((K, R, FS, width), bf16),
                pltpu.VMEM(master.shape, jnp.float32),
                pltpu.VMEM(momentum.shape, jnp.float32),
                pltpu.VMEM((2, R * F, sub, width), jnp.int32),
                pltpu.VMEM((2, R * F, sub, blocks), jnp.float32),
                pltpu.SemaphoreType.DMA((6, K)),
                pltpu.SemaphoreType.DMA((6, K)),
                pltpu.SemaphoreType.DMA((2, 2)),
                pltpu.SemaphoreType.DMA((2,)),
                pltpu.SemaphoreType.DMA((2 + R, K)),
            ],
            compiler_params=pltpu.CompilerParams(
                collective_id=0, has_side_effects=True, vmem_limit_bytes=60 * 1024 * 1024
            ),
        )(codes, scales, master, momentum)
        return (new_master, new_momentum, weights.reshape(total_rows, width))

    return jax.shard_map(
        local,
        mesh=mesh,
        in_specs=(
            P("replica", None, "fsdp"),
            P("replica", "fsdp", None),
            P(("replica", "fsdp"), None),
            P(("replica", "fsdp"), None),
        ),
        out_specs=(P(("replica", "fsdp"), None), P(("replica", "fsdp"), None), P(None, "fsdp")),
        check_vma=False,
    )
```

time: 349 us -> 186 us (0.53)
  waiting for transfers between devices: 201 us -> 0 us
  Pallas kernels: 0 us -> 168 us
  blocking collectives: 52.5 us -> 0 us
  local copies, waits for them, and re-layouts: 55 us -> 17.6 us
  other arithmetic: 21 us -> 0 us
  between operations: 14.1 us -> 0.65 us
  starting transfers between devices: 4.69 us -> 0 us
    pallas_call x0 -> x1, Pallas kernels: none -> 168 us  [local(): pl.pallas_call(functools.partial(kernel, (A, B, F, K, sub, width, blocks)...]
    reduce_scatter x1 -> x0, waiting for transfers between devices: 89.2 us -> none  [local(): lax.psum_scatter(delta_local.astype(jnp.bfloat16), 'replica', scatter_dim...]
    all_gather x1 -> x0, waiting for transfers between devices: 74 us -> none  [local(): weights = lax.all_gather(columns, 'replica', axis=0, tiled=True)]
    all_to_all x1 -> x0, blocking collectives: 52.5 us -> none  [local(): lax.all_to_all(rounded, 'fsdp', split_axis=1, concat_axis=0, tiled=True)]
    all_to_all x1 -> x0, waiting for transfers between devices: 37.8 us -> none  [local(): lax.all_to_all(partial_sum.astype(jnp.bfloat16), 'fsdp', split_axis=0, co...]
    convert_element_type x2 -> x0, other arithmetic: 18.9 us -> none  [the longest x1 11.6 us: local(): delta_local.astype(jnp.bfloat16)]
    unnamed x7 -> x5, local copies, waits for them, and re-layouts: 30.8 us -> 14.1 us
    mul x1 -> x0, local copies, waits for them, and re-layouts: 15.9 us -> none  [dequantize(): scaled * jnp.transpose(scales[0])[:, :, None]]
  transfers between devices with their start and end apart: 3 -> 0, of which waited for: 3 -> 0; matrix products, arithmetic and copies ran while one was open for 7% -> 0% of each run, Pallas kernels for 0% -> 0%
where the time goes in v1:
time: 186 us
  Pallas kernels  168 us (90%)
  local copies, waits for them, and re-layouts  17.6 us (9%)
    pallas_call x1, Pallas kernels, local(): pl.pallas_call(functools.partial(kernel, (A, B, F, K, sub, width, blocks)...  168 us
    unnamed x5, local copies, waits for them, and re-layouts  14.1 us

profile of v1, /device:TPU:0, one launch (start us, length us, event | category | flops | bytes accessed | tf_op | source)
XLA Modules:
  0.0 186.0 jit_solution(9173074186235303740)
XLA Ops:
  0.6 3.5 %copy.7 = f32[8192,4]{1,0:T(8,128)} copy(f32[8192,4]{0,1:T(4,128)} %bitcast.9) | data formatting | bytes 262144 | tf_op jit(solution)/shard_map/transpose | solution.py:298
  4.1 167.7 %shard_map.67 = (f32[256,4096]{1,0:T(8,128)}, f32[256,4096]{1,0:T(8,128)}, bf16[32,8,32,512]{3,2,1,0:T(8,128)(2,1)}) custom-call(s32[32,8,32,512]{3,2,1,0:T(8,128)} %bitcast.6, f32[32,8,32,4]{3,2,1,0:T(8,128)} %bitcast.7, f32[256,4096]{1,0:T(8,128)} %master.1, f32[256,4096]{1,0:T(8,128)} %momentum.1), custom_call_target="tpu_custom_call" | custom-call | tf_op jit(solution)/shard_map/pallas_call | solution.py:301
  171.9 0.0 copy-start
  171.9 4.8 %copy.11 = f32[256,4096]{1,0:T(8,128)} copy(f32[256,4096]{1,0:T(8,128)} %get-tuple-element.12) | data formatting | bytes 8388608
  176.7 0.0 copy-done
  176.7 2.0 %copy.12 = f32[256,4096]{1,0:T(8,128)} copy(f32[256,4096]{1,0:T(8,128)S(1)} %copy-done) | data formatting | bytes 8388608
  178.7 7.3 %copy.13 = bf16[8192,512]{1,0:T(8,128)(2,1)} copy(bf16[8192,512]{1,0:T(8,128)(2,1)} %bitcast.8) | data formatting | bytes 16777216
Async XLA Ops:
  171.9 4.8 %copy-start = (f32[256,4096]{1,0:T(8,128)S(1)}, f32[256,4096]{1,0:T(8,128)}, u32[]{:S(2)}) copy-start(f32[256,4096]{1,0:T(8,128)} %get-tuple-element.13) | copy-start | bytes 12582916

commit v2 on v1

--- a/solution.py
+++ b/solution.py
@@ -12,13 +12,13 @@
 outer_rate = 0.7
 momentum_factor = 0.9
 
-LAGS = (0, 2, 3, 4, 5, 6, 7)
+LAGS = (0, 2, 4, 6, 8, 10, 12)
 RS1, RS2, X1, X2, AG1, AG2 = range(6)
 
 
 def kernel(cfg, codes, scales, master, momentum, new_master, new_momentum, weights,
-           delta, rs1e, rs1o, rs2e, rs2o, part, got, wsend, wbuf, mast, mom, cbuf, sbuf,
-           send_sem, recv_sem, in_sem, state_sem, out_sem):
+           delta, rs1e, rs1o, rs2e, rs2o, part, got, wsend, mast, mom, cbuf, flat, sbuf,
+           send_sem, recv_sem, in_sem, state_sem, out_sem, own_sem):
     A, B, F, K, sub, width, blocks = cfg
     R, FS, block = A * B, F * sub, width // blocks
     r, f = lax.axis_index("replica"), lax.axis_index("fsdp")
@@ -35,11 +35,10 @@
 
     def load(k):
         slot = lax.rem(k, 2)
-        return (
-            pltpu.make_async_copy(codes.at[:, k], cbuf.at[slot], in_sem.at[0, slot]),
-            pltpu.make_async_copy(scales.at[:, k], sbuf.at[slot], in_sem.at[1, slot]),
-        )
-
+        return (pltpu.make_async_copy(codes.at[:, k], cbuf.at[slot], in_sem.at[slot]),)
+
+    scales_in = pltpu.make_async_copy(scales.at[0], flat.at[pl.ds(0, blocks)], state_sem.at[2])
+    scales_in.start()
     for k in range(min(2, K)):
         for copy in load(k):
             copy.start()
@@ -57,6 +56,14 @@
         pl.semaphore_signal(barrier, inc=1, device_id=(a * B + b_peer(i), f), device_id_type=MESH)
     for i in range(F - 1):
         pl.semaphore_signal(barrier, inc=1, device_id=(r, f_peer(i)), device_id_type=MESH)
+    scales_in.wait()
+
+    def turn(i, carry):
+        tile = flat[:, pl.ds(pl.multiple_of(i * 128, 128), 128)]
+        sbuf[pl.ds(pl.multiple_of(i * 128, 128), 128), :] = jnp.transpose(tile)
+        return carry
+
+    lax.fori_loop(0, flat.shape[1] // 128, turn, 0, unroll=8)
     pl.semaphore_wait(barrier, A + B + F - 3)
 
     def send(stage, k, src, dst, device):
@@ -104,11 +111,11 @@
             q, j = g // F, lax.rem(g, F)
             for n in range(blocks):
                 cols = pl.ds(n * block, block)
-                value = f32(cbuf[slot, g, :, cols]) * sbuf[slot, g, :, pl.ds(n, 1)]
+                value = f32(cbuf[slot, g, :, cols]) * sbuf[pl.ds(pl.multiple_of((g * K + k) * sub, sub), sub), pl.ds(n, 1)]
                 delta[k, q, rows(j), cols] = value.astype(jnp.bfloat16)
             return carry
 
-        lax.fori_loop(0, R * F, one, 0)
+        lax.fori_loop(0, R * F, one, 0, unroll=4)
 
         @pl.when(k + 2 < K)
         def _():
@@ -143,7 +150,7 @@
                     buf[k // 2, 0, q, rows(j), :] = total.astype(jnp.bfloat16)
                     return carry
 
-                lax.fori_loop(0, F, add, 0)
+                lax.fori_loop(0, F, add, 0, unroll=4)
                 dst = rs2e if even else rs2o
                 send(RS2, k, buf.at[k // 2, 0, q], dst.at[k // 2, peers - 1 - i], (target, f))
 
@@ -165,7 +172,7 @@
                 part[k, rows(j), :] = total.astype(jnp.bfloat16)
                 return carry
 
-            lax.fori_loop(0, F, add, 0)
+            lax.fori_loop(0, F, add, 0, unroll=4)
 
         by_parity(k, go)
 
@@ -183,6 +190,9 @@
             pltpu.make_async_copy(mast.at[span], new_master.at[span], out_sem.at[0, k]),
             pltpu.make_async_copy(mom.at[span], new_momentum.at[span], out_sem.at[1, k]),
         )
+
+    def own(k):
+        return pltpu.make_async_copy(wsend.at[k, rows(f)], weights.at[r * F + f, k], own_sem.at[k])
 
     def stage3(k):
         @pl.when(k == 0)
@@ -203,23 +213,24 @@
             wsend[k, rows(j), :] = p.astype(jnp.bfloat16)
             return carry
 
-        lax.fori_loop(0, F, update, 0)
+        lax.fori_loop(0, F, update, 0, unroll=4)
 
         def out(i, carry):
             j = f_peer(i)
-            send(X2, k, wsend.at[k, rows(j)], wbuf.at[k, r, rows(f)], (r, j))
+            send(X2, k, wsend.at[k, rows(j)], weights.at[r * F + f, k], (r, j))
             return carry
 
         lax.fori_loop(0, F - 1, out, 0)
-        wbuf[k, r, rows(f), :] = wsend[k, rows(f), :]
+        own(k).start()
         for copy in results(k):
             copy.start()
 
     def stage4(k):
         wait_bytes(recv_sem, X2, k, amount(X2, k, True))
-
-        def go(even):
-            here = wbuf.at[k, r]
+        own(k).wait()
+
+        def go(even):
+            here = weights.at[pl.ds(r * F, F), k]
             for i in range(B - 1 if even else A - 1):
                 target = a * B + b_peer(i) if even else a_peer(i) * B + b
                 send(AG1, k, here, here, (target, f))
@@ -230,26 +241,19 @@
         def go(even):
             wait_bytes(recv_sem, AG1, k, amount(AG1, k, even))
             if even:
-                here = wbuf.at[k, pl.ds(a * B, B)]
+                here = weights.at[pl.ds(a * B * F, B * F), k]
                 for i in range(A - 1):
                     send(AG2, k, here, here, (a_peer(i) * B + b, f))
             else:
                 for i in range(B - 1):
                     for aa in range(A):
-                        here = wbuf.at[k, aa * B + b]
+                        here = weights.at[pl.ds((aa * B + b) * F, F), k]
                         send(AG2, k, here, here, (a * B + b_peer(i), f))
 
         by_parity(k, go)
-
-    def columns(k, q):
-        return pltpu.make_async_copy(
-            wbuf.at[k, q].reshape(F, sub, width), weights.at[pl.ds(q * F, F), k], out_sem.at[2 + q, k]
-        )
 
     def stage6(k):
         by_parity(k, lambda even: wait_bytes(recv_sem, AG2, k, amount(AG2, k, even)))
-        for q in range(R):
-            columns(k, q).start()
 
     stages = (stage0, stage1, stage2, stage3, stage4, stage5, stage6)
 
@@ -268,8 +272,6 @@
     def finish(k, carry):
         for copy in results(k):
             copy.wait()
-        for q in range(R):
-            columns(k, q).wait()
 
         def go(even):
             for stage in range(6):
@@ -290,20 +292,20 @@
         total_rows, width = codes.shape[1:]
         blocks = scales.shape[1]
         own = total_rows // (R * F)
-        sub = 32 if own % 32 == 0 else own
+        sub = 16 if own % 16 == 0 else own
         K = own // sub
         FS = F * sub
         even, odd = (K + 1) // 2, max(1, K // 2)
         codes = codes.reshape(R * F, K, sub, width)
-        scales = jnp.transpose(scales[0]).reshape(R * F, K, sub, blocks)
+        lines = max(8, blocks)
         any_spec = pl.BlockSpec(memory_space=pl.ANY)
         bf16 = jnp.bfloat16
         new_master, new_momentum, weights = pl.pallas_call(
             functools.partial(kernel, (A, B, F, K, sub, width, blocks)),
             out_shape=(
-                jax.ShapeDtypeStruct(master.shape, jnp.float32),
-                jax.ShapeDtypeStruct(momentum.shape, jnp.float32),
-                jax.ShapeDtypeStruct((R * F, K, sub, width), bf16),
+                pltpu.VMEM(master.shape, jnp.float32),
+                pltpu.VMEM(momentum.shape, jnp.float32),
+                pltpu.VMEM((R * F, K, sub, width), bf16),
             ),
             in_specs=[any_spec] * 4,
             out_specs=(any_spec,) * 3,
@@ -316,19 +318,20 @@
                 pltpu.VMEM((K, FS, width), bf16),
                 pltpu.VMEM((K, FS, width), bf16),
                 pltpu.VMEM((K, FS, width), bf16),
-                pltpu.VMEM((K, R, FS, width), bf16),
                 pltpu.VMEM(master.shape, jnp.float32),
                 pltpu.VMEM(momentum.shape, jnp.float32),
                 pltpu.VMEM((2, R * F, sub, width), jnp.int32),
-                pltpu.VMEM((2, R * F, sub, blocks), jnp.float32),
+                pltpu.VMEM((lines, total_rows), jnp.float32),
+                pltpu.VMEM((total_rows, lines), jnp.float32),
                 pltpu.SemaphoreType.DMA((6, K)),
                 pltpu.SemaphoreType.DMA((6, K)),
-                pltpu.SemaphoreType.DMA((2, 2)),
                 pltpu.SemaphoreType.DMA((2,)),
-                pltpu.SemaphoreType.DMA((2 + R, K)),
+                pltpu.SemaphoreType.DMA((3,)),
+                pltpu.SemaphoreType.DMA((2, K)),
+                pltpu.SemaphoreType.DMA((K,)),
             ],
             compiler_params=pltpu.CompilerParams(
-                collective_id=0, has_side_effects=True, vmem_limit_bytes=60 * 1024 * 1024
+                collective_id=0, has_side_effects=True, vmem_limit_bytes=40 * 1024 * 1024
             ),
         )(codes, scales, master, momentum)
         return (new_master, new_momentum, weights.reshape(total_rows, width))

time: 186 us -> 157 us (0.84)
  Pallas kernels: 168 us -> 149 us
  local copies, waits for them, and re-layouts: 17.6 us -> 7.42 us
    pallas_call x1, Pallas kernels: 168 us -> 149 us  [local(): pl.pallas_call(functools.partial(kernel, (A, B, F, K, sub, width, blocks)...]
    unnamed x5 -> x3, local copies, waits for them, and re-layouts: 14.1 us -> 7.42 us
    transpose x1 -> x0, local copies, waits for them, and re-layouts: 3.5 us -> none  [local(): scales = jnp.transpose(scales[0]).reshape(R * F, K, sub, blocks)]
where the time goes in v2:
time: 157 us
  Pallas kernels  149 us (95%)
  local copies, waits for them, and re-layouts  7.42 us (5%)
    pallas_call x1, Pallas kernels, local(): pl.pallas_call(functools.partial(kernel, (A, B, F, K, sub, width, blocks)...  149 us
    unnamed x3, local copies, waits for them, and re-layouts  7.42 us

profile of v2, /device:TPU:0, one launch (start us, length us, event | category | flops | bytes accessed | tf_op | source)
XLA Modules:
  0.0 156.9 jit_solution(5425350073245399194)
XLA Ops:
  0.6 148.9 %shard_map.67 = (f32[256,4096]{1,0:T(8,128)S(1)}, f32[256,4096]{1,0:T(8,128)S(1)}, bf16[32,16,16,512]{3,2,1,0:T(8,128)(2,1)S(1)}) custom-call(s32[32,16,16,512]{3,2,1,0:T(8,128)} %bitcast.3, f32[1,4,8192]{2,1,0:T(4,128)} %scales.1, f32[256,4096]{1,0:T(8,128)} %master.1, f32[256,4096]{1,0:T(8,128)} %momentum.1), custom_call_target="tpu_custom_call" | custom-call | tf_op jit(solution)/shard_map/pallas_call | solution.py:303
  149.5 2.0 %copy.10 = f32[256,4096]{1,0:T(8,128)} copy(f32[256,4096]{1,0:T(8,128)S(1)} %get-tuple-element.9) | data formatting | bytes 8388608
  151.5 2.0 %copy.11 = f32[256,4096]{1,0:T(8,128)} copy(f32[256,4096]{1,0:T(8,128)S(1)} %get-tuple-element.10) | data formatting | bytes 8388608
  153.5 3.4 %copy.12 = bf16[8192,512]{1,0:T(8,128)(2,1)} copy(bf16[8192,512]{1,0:T(8,128)(2,1)S(1)} %bitcast.2) | data formatting | bytes 16777216
